TPU v7x, 32 devices: a whole 2x2x4 slice. The times are simulated.
32 devices in a mesh: section: 4 (over y, x), tensor: 2 (over core), dp: 4 (over z).
Axes of the slice: x: 2, y: 2, z: 4, core: 2. Of those that a mesh axis runs over, the one named last changes fastest.
Arguments:
- hidden_in: bfloat16 [128, 4096], P('dp', 'tensor'), may hold values from -6 to 6
- norm_gain: float32 [4, 4096], P('section'), may hold values from 0.25 to 1.75
- gate_weight: bfloat16 [4, 4096, 8192], P('section', 'dp', 'tensor'), may hold values from -0.09375 to 0.09375
- up_weight: bfloat16 [4, 4096, 8192], P('section', 'dp', 'tensor'), may hold values from -0.09375 to 0.09375
- down_weight: bfloat16 [4, 4096, 8192], P('section', 'dp', 'tensor'), may hold values from -0.0625 to 0.0625
- lengths: int32 [16], P('dp'), may hold values from 3 to 8
Outputs:
- rdm: float32 [4, 16, 16], P('section', 'dp')
Inputs may be any that keep to these rules, and one draw needn't show every extreme that they name: `lengths`: the number of leading valid token rows of each sentence.
All inputs are finite; a program needn't handle non-finite values.
Results may differ from a plain program's by a relative error of at most 0.0012.
Values may be sent and summed in bfloat16 or wider, within the bound.
A program may use at most 192 MiB of HBM per device.

v0:
```python
import functools

import jax
import jax.numpy as jnp
from jax import lax
from jax.experimental import pallas as pl
from jax.experimental.pallas import tpu as pltpu
from jax.sharding import PartitionSpec as P

RMS_EPS = 1e-05
UNIT_FLOOR = 0.1
CONTRACT_LAST = (((1,), (1,)), ((), ()))
MESH = pl.DeviceIdType.MESH
LANES = 128
F32 = jnp.float32
BF16 = jnp.bfloat16


SPLIT = 2


def pieces(fc):
    return 2 if fc % (2 * LANES) == 0 else 1


def kernel(dps, tensors, sections, hidden_ref, gain_ref, lens_ref, gate_hbm, up_hbm, down_hbm,
           out_ref, gate_v, up_v, down_v, x_in, rs_out, rs_in, own_gu, own_ss, hid, tx, outs, gram, lbuf, lens_full,
           w_sem, d_send, x_send, x_recv, rs_send, rs_recv, h_send, h_recv, t_send, t_recv,
           g_send, g_recv, l_send, l_recv):
    section = lax.axis_index("section")
    tensor = lax.axis_index("tensor")
    dp = lax.axis_index("dp")
    micros = dps * SPLIT
    width = gate_v.shape[0]
    cols = gate_v.shape[1]
    fc = cols // dps
    halves = pieces(fc)
    fh = fc // halves
    rows = x_in.shape[1]
    d_model = width * dps
    nj = hidden_ref.shape[1] // width

    def chunk(c):
        return pl.ds(pl.multiple_of(c * fc, fc), fc)

    def wcopy(which, c):
        src, dst = ((gate_hbm, gate_v), (up_hbm, up_v), (down_hbm, down_v))[which]
        return pltpu.make_async_copy(src.at[0, :, chunk(c)], dst.at[:, chunk(c)], w_sem.at[which, c])

    if dps == 4:
        mirror = dps - 1 - dp
        peers = [mirror, lax.rem(dp + 2, dps), lax.rem(mirror + 2, dps)]
    else:
        peers = [lax.rem(dp + k, dps) for k in range(1, dps)]
    order = peers + [dp]
    for c in order:
        wcopy(0, c).start()
        wcopy(1, c).start()
    for c in order:
        wcopy(2, c).start()

    barrier = pltpu.get_barrier_semaphore()
    for kt in range(tensors):
        for kd in range(dps):
            if kt or kd:
                pl.semaphore_signal(
                    barrier, inc=1,
                    device_id={"tensor": lax.rem(tensor + kt, tensors), "dp": lax.rem(dp + kd, dps)},
                    device_id_type=MESH)

    @pl.when(section > 0)
    def _():
        pl.semaphore_signal(barrier, inc=1, device_id={"section": section - 1}, device_id_type=MESH)

    @pl.when(section < sections - 1)
    def _():
        pl.semaphore_signal(barrier, inc=1, device_id={"section": section + 1}, device_id_type=MESH)

    pl.semaphore_wait(
        barrier,
        tensors * dps + 1 - jnp.where(section == 0, 1, 0) - jnp.where(section == sections - 1, 1, 0))

    each = lens_ref.shape[0]
    sents = each * dps
    slot = lax.broadcasted_iota(jnp.int32, lbuf.shape[1:], 0)
    own_lens = jnp.ones(lbuf.shape[1:], F32)
    for n in range(each):
        own_lens = jnp.where(slot == n, lens_ref[n].astype(F32), own_lens)
    lbuf[dp] = own_lens

    def s_copy(buf, send, recv, c, peer):
        return pltpu.make_async_remote_copy(
            src_ref=buf.at[c], dst_ref=buf.at[c], send_sem=send.at[peer], recv_sem=recv.at[c],
            device_id={"dp": peer}, device_id_type=MESH)

    def spread(h, j, k):
        return pltpu.make_async_remote_copy(
            src_ref=hidden_ref.at[pl.ds(h * rows, rows), pl.ds(j * width, width)],
            dst_ref=x_in.at[dp * SPLIT + h],
            send_sem=d_send.at[h, j * tensors + k], recv_sem=x_recv.at[dp * SPLIT + h],
            device_id={"tensor": lax.rem(tensor + k, tensors), "dp": tensor * nj + j}, device_id_type=MESH)

    @pl.when(section == 0)
    def _():
        for h in range(SPLIT):
            for j in range(nj):
                for k in range(tensors):
                    if k:
                        spread(h, j, k).start()
                    else:
                        @pl.when(tensor * nj + j != dp)
                        def _():
                            spread(h, j, k).start()

                        @pl.when(tensor * nj + j == dp)
                        def _():
                            x_in[dp * SPLIT + h] = hidden_ref[h * rows:(h + 1) * rows, j * width:(j + 1) * width]

    for c in peers:
        s_copy(lbuf, l_send, l_recv, dp, c).start()

    def base(q):
        return LANES + 2 * fh * q

    def piece(q):
        return pl.ds(0, base(1)) if q == 0 else pl.ds(base(q), 2 * fh)

    def rs_copy(m, c, q):
        return pltpu.make_async_remote_copy(
            src_ref=rs_out.at[m, c, :, piece(q)], dst_ref=rs_in.at[m, dp, :, piece(q)],
            send_sem=rs_send.at[m, c * halves + q], recv_sem=rs_recv.at[m, dp * halves + q],
            device_id={"dp": c}, device_id_type=MESH)

    def rs_wait(m, c, q):
        return pltpu.make_async_remote_copy(
            src_ref=rs_out.at[m, c, :, piece(q)], dst_ref=rs_in.at[m, c, :, piece(q)],
            send_sem=rs_send.at[m, c * halves + q], recv_sem=rs_recv.at[m, c * halves + q],
            device_id={"dp": c}, device_id_type=MESH)

    def h_copy(m, c, peer, q):
        part = hid.at[m, c, :, pl.ds(q * fh, fh)]
        return pltpu.make_async_remote_copy(
            src_ref=part, dst_ref=part,
            send_sem=h_send.at[m, peer * halves + q], recv_sem=h_recv.at[m, c * halves + q],
            device_id={"dp": peer}, device_id_type=MESH)

    def columns(c, q):
        return pl.ds(pl.multiple_of(c * fc + q * fh, fh), fh)

    def t_copy(m, c, peer):
        return pltpu.make_async_remote_copy(
            src_ref=tx.at[m, c], dst_ref=tx.at[m, c],
            send_sem=t_send.at[m, peer], recv_sem=t_recv.at[m, c],
            device_id={"tensor": peer}, device_id_type=MESH)

    def x_copy(m, to):
        return pltpu.make_async_remote_copy(
            src_ref=outs.at[m], dst_ref=x_in.at[m],
            send_sem=x_send.at[m], recv_sem=x_recv.at[m],
            device_id={"section": to}, device_id_type=MESH)

    lane = lax.broadcasted_iota(jnp.int32, (rows, LANES), 1)

    def gate_up(m):
        local = jnp.logical_and(section == 0, jnp.logical_and(m // SPLIT == dp, dp // nj == tensor))

        @pl.when(jnp.logical_not(local))
        def _():
            x_copy(m, section).wait_recv()

        x = x_in[m].astype(F32)
        ss = jnp.sum(x * x, axis=1, keepdims=True)
        high = ss.astype(BF16)
        low = (ss - high.astype(F32)).astype(BF16)
        packed = jnp.where(lane < LANES // 2, high.astype(F32), low.astype(F32)).astype(BF16)
        own_ss[m] = jnp.broadcast_to(ss, (rows, LANES))
        scaled = (x * gain_ref[:, pl.ds(pl.multiple_of(dp * width, width), width)]).astype(BF16)
        for c, q in [(c, q) for q in range(halves) for c in peers] + [(dp, q) for q in range(halves)]:
            if q == 0:
                @pl.when(m == 0)
                def _():
                    wcopy(0, c).wait()
                    wcopy(1, c).wait()

            g = jnp.dot(scaled, gate_v[:, columns(c, q)], preferred_element_type=F32)
            u = jnp.dot(scaled, up_v[:, columns(c, q)], preferred_element_type=F32)
            at = base(q)
            if c is not dp:
                if q == 0:
                    rs_out[m, c, :, 0:LANES] = packed
                rs_out[m, c, :, at:at + fh] = g.astype(BF16)
                rs_out[m, c, :, at + fh:at + 2 * fh] = u.astype(BF16)
                rs_copy(m, c, q).start()
            else:
                own_gu[m, :, q * 2 * fh:q * 2 * fh + fh] = g
                own_gu[m, :, q * 2 * fh + fh:(q + 1) * 2 * fh] = u

    def activate(m):
        inv = None
        for q in range(halves):
            for c in peers:
                rs_wait(m, c, q).wait_recv()
            if q == 0:
                ss = own_ss[m][:, 0:1]
                for c in peers:
                    ss = ss + jnp.sum(rs_in[m, c, :, 0:LANES].astype(F32), axis=1, keepdims=True) * (2.0 / LANES)
                inv = lax.rsqrt(ss * (1.0 / d_model) + RMS_EPS)
            g = own_gu[m, :, q * 2 * fh:q * 2 * fh + fh]
            u = own_gu[m, :, q * 2 * fh + fh:(q + 1) * 2 * fh]
            at = base(q)
            for c in peers:
                g = g + rs_in[m, c, :, at:at + fh].astype(F32)
                u = u + rs_in[m, c, :, at + fh:at + 2 * fh].astype(F32)
            g = g * inv
            u = u * inv
            hid[m, dp, :, q * fh:(q + 1) * fh] = (g / (1.0 + jnp.exp(-g)) * u).astype(BF16)
            for c in peers:
                h_copy(m, dp, c, q).start()

    def finish(m):
        acc = jnp.zeros((rows, width), F32)
        arrivals = [(dp, q) for q in range(halves)]
        arrivals += [(c, q) for q in range(halves) for c in peers[::2] + peers[1::2]]
        for c, q in arrivals:
            if c is not dp:
                h_copy(m, c, c, q).wait_recv()
            if q == 0:
                @pl.when(m == 0)
                def _():
                    wcopy(2, c).wait()

            acc = acc + lax.dot_general(hid[m, c, :, q * fh:(q + 1) * fh], down_v[:, columns(c, q)],
                                        CONTRACT_LAST, preferred_element_type=F32)
        tx[m, tensor] = acc.astype(BF16)
        for k in range(1, tensors):
            t_copy(m, tensor, lax.rem(tensor + k, tensors)).start()
        for k in range(1, tensors):
            other = lax.rem(tensor + k, tensors)
            t_copy(m, other, other).wait_recv()
        total = tx[m, 0].astype(F32)
        for t in range(1, tensors):
            total = total + tx[m, t].astype(F32)
        outs[m] = (x_in[m].astype(F32) + total).astype(BF16)

        @pl.when(section < sections - 1)
        def _():
            x_copy(m, section + 1).start()

    def step(i, carry):
        @pl.when(i < micros)
        def _():
            gate_up(i)

        @pl.when(i > 0)
        def _():
            finish(i - 1)

        @pl.when(i < micros)
        def _():
            activate(i)
        return carry

    lax.fori_loop(0, micros + 1, step, 0)

    for c in peers:
        s_copy(lbuf, l_send, l_recv, c, c).wait_recv()
    for c in range(dps):
        lens_full[c * each:(c + 1) * each] = lbuf[c, 0:each]
    tokens = micros * rows
    per = tokens // sents
    place = lax.broadcasted_iota(jnp.int32, (sents, tokens), 1) - per * lax.broadcasted_iota(
        jnp.int32, (sents, tokens), 0)
    lens = lens_full[:, 0:1]
    valid = jnp.logical_and(place >= 0, place.astype(F32) < lens)
    mask = jnp.where(valid, 1.0, 0.0).astype(BF16)
    pooled = jnp.dot(mask, outs[...].reshape(tokens, width), preferred_element_type=F32) / lens

    def share(buf, send, recv):
        for c in peers:
            s_copy(buf, send, recv, dp, c).start()
        for c in peers:
            s_copy(buf, send, recv, c, c).wait_recv()

    mean = jnp.sum(pooled, axis=1, keepdims=True) * (1.0 / width)
    centered = pooled - mean
    narrow = centered.astype(BF16)
    sq = jnp.sum(centered * centered, axis=1, keepdims=True)
    gram[dp, 0] = jnp.zeros((sents, LANES), F32)
    gram[dp, 0, :, 0:sents] = lax.dot_general(narrow, narrow, CONTRACT_LAST, preferred_element_type=F32)
    gram[dp, 1] = jnp.broadcast_to(sq, (sents, LANES))
    gram[dp, 2] = jnp.broadcast_to(mean, (sents, LANES))
    share(gram, g_send, g_recv)
    products, sq, mean = gram[0, 0], gram[0, 1], gram[0, 2]
    for c in range(1, dps):
        products = products + gram[c, 0]
        sq = sq + gram[c, 1]
        mean = mean + gram[c, 2]
    mean = mean * (1.0 / dps)
    r_i = lax.broadcasted_iota(jnp.int32, (sents, LANES), 0)
    c_i = lax.broadcasted_iota(jnp.int32, (sents, LANES), 1)
    for c in range(dps):
        off = gram[c, 2] - mean
        off_row = jnp.sum(jnp.where(r_i == c_i, off, 0.0), axis=0, keepdims=True)
        products = products + off * off_row * float(width)
        sq = sq + off * off * float(width)
    scale = lax.rsqrt(sq * (1.0 / d_model) + UNIT_FLOOR)
    across = jnp.sum(jnp.where(r_i == c_i, scale, 0.0), axis=0, keepdims=True)
    whole = 1.0 - products * scale * across * (1.0 / d_model)
    for r in range(each):
        row = jnp.sum(jnp.where(r_i == dp * each + r, whole, 0.0), axis=0, keepdims=True)
        out_ref[0, r:r + 1, :] = row[:, 0:sents]

    @pl.when(section == 0)
    def _():
        for h in range(SPLIT):
            for j in range(nj):
                for k in range(tensors):
                    if k:
                        spread(h, j, k).wait_send()
                    else:
                        @pl.when(tensor * nj + j != dp)
                        def _():
                            spread(h, j, k).wait_send()

    def drain(m, carry):
        for c in peers:
            for q in range(halves):
                rs_copy(m, c, q).wait_send()
                h_copy(m, dp, c, q).wait_send()
        for k in range(1, tensors):
            t_copy(m, tensor, lax.rem(tensor + k, tensors)).wait_send()

        @pl.when(section < sections - 1)
        def _():
            x_copy(m, section + 1).wait_send()
        return carry

    lax.fori_loop(0, micros, drain, 0)
    for c in peers:
        s_copy(lbuf, l_send, l_recv, dp, c).wait_send()
        s_copy(gram, g_send, g_recv, dp, c).wait_send()


def per_device(hidden_in, norm_gain, gate_weight, up_weight, down_weight, lengths):
    sections = lax.axis_size("section")
    tensors = lax.axis_size("tensor")
    dps = lax.axis_size("dp")
    _, width, cols = gate_weight.shape
    micros = dps * SPLIT
    rows = hidden_in.shape[0] // SPLIT
    fc = cols // dps
    halves = pieces(fc)
    nj = hidden_in.shape[1] // width
    each = lengths.shape[0]
    sents = each * dps
    vm = pl.BlockSpec(memory_space=pltpu.VMEM)
    hbm = pl.BlockSpec(memory_space=pl.ANY)
    dma = pltpu.SemaphoreType.DMA
    smem = pl.BlockSpec(memory_space=pltpu.SMEM)
    return pl.pallas_call(
        functools.partial(kernel, dps, tensors, sections),
        out_shape=jax.ShapeDtypeStruct((1, each, sents), F32),
        in_specs=[vm] * 2 + [smem] + [hbm] * 3,
        out_specs=vm,
        scratch_shapes=[
            pltpu.VMEM((width, cols), BF16),
            pltpu.VMEM((width, cols), BF16),
            pltpu.VMEM((width, cols), BF16),
            pltpu.VMEM((micros, rows, width), BF16),
            pltpu.VMEM((micros, dps, rows, 2 * fc + LANES), BF16),
            pltpu.VMEM((micros, dps, rows, 2 * fc + LANES), BF16),
            pltpu.VMEM((micros, rows, 2 * fc), F32),
            pltpu.VMEM((micros, rows, LANES), F32),
            pltpu.VMEM((micros, dps, rows, fc), BF16),
            pltpu.VMEM((micros, tensors, rows, width), BF16),
            pltpu.VMEM((micros, rows, width), BF16),
            pltpu.VMEM((dps, 3, sents, LANES), F32),
            pltpu.VMEM((dps, -(-each // 8) * 8, LANES), F32),
            pltpu.VMEM((sents, LANES), F32),
            dma((3, dps)),
            dma((SPLIT, nj * tensors)),
            dma((micros,)),
            dma((micros,)),
            dma((micros, dps * halves)),
            dma((micros, dps * halves)),
            dma((micros, dps * halves)),
            dma((micros, dps * halves)),
            dma((micros, tensors)),
            dma((micros, tensors)),
            dma((dps,)),
            dma((dps,)),
            dma((dps,)),
            dma((dps,)),
        ],
        compiler_params=pltpu.CompilerParams(
            collective_id=0, has_side_effects=True, vmem_limit_bytes=60 * 1024 * 1024),
    )(hidden_in, norm_gain, lengths, gate_weight, up_weight, down_weight)


def solution(mesh):
    placed = (
        P("dp", "tensor"),
        P("section", None),
        P("section", "dp", "tensor"),
        P("section", "dp", "tensor"),
        P("section", "dp", "tensor"),
        P("dp"),
    )
    return jax.shard_map(
        per_device, mesh=mesh, in_specs=placed, out_specs=P("section", "dp", None), check_vma=False
    )
```

profile of v0, /device:TPU:7, one launch (start us, length us, event | category | flops | bytes accessed | tf_op | source)
XLA Modules:
  0.0 151.6 jit_solution(12221841907211932651)
XLA Ops:
  0.0 150.3 %shard_map.64 = f32[1,4,16]{2,1,0:T(4,128)} custom-call(bf16[32,2048]{1,0:T(8,128)(2,1)} %hidden_ref.1, f32[1,4096]{1,0:T(1,128)} %gain_ref.1, s32[4]{0:T(128)} %lens_ref.1, bf16[1,1024,4096]{2,1,0:T(8,128)(2,1)} %gate_hbm.1, bf16[1,1024,4096]{2,1,0:T(8,128)(2,1)} %up_hbm.1, bf16[1,1024,4096]{2,1,0:T(8,128)(2,1)} %down_hbm.1), custom_call_target="tpu_custom_call" | custom-call | tf_op jit(solution)/shard_map/pallas_call | solution.py:360
  150.4 1.3 copy.8
where the time goes:
time: 152 us
  Pallas kernels  150 us (99%)
    pallas_call x1, Pallas kernels, per_device(): pl.pallas_call(functools.partial(kernel, dps, tensors, sections), out_sha...  150 us

commit v1 on v0

v1 whole, which is shorter than its diff:
```python
import functools

import jax
import jax.numpy as jnp
from jax import lax
from jax.experimental import pallas as pl
from jax.experimental.pallas import tpu as pltpu
from jax.sharding import PartitionSpec as P

RMS_EPS = 1e-05
UNIT_FLOOR = 0.1
CONTRACT_LAST = (((1,), (1,)), ((), ()))
MESH = pl.DeviceIdType.MESH
LANES = 128
F32 = jnp.float32
BF16 = jnp.bfloat16

SPLIT = 2
Q = 2
AHEAD = 2

LEAF = (("G", (0, 1, 2, 3), 0), ("F", ((0, 0), (1, 0), (0, 1), (1, 1)), 1), ("E", None, 2))
HUB = (("G", (0, 1), 0), ("A", 0, 1), ("G", (2, 3), 0), ("A", 1, 1), ("C", 0, 0), ("F", ((0, 0), (0, 1)), 1),
       ("C", 1, 0), ("F", ((1, 0), (1, 1)), 1), ("E", None, 2))


def kernel(dps, tensors, sections, hidden_ref, gain_ref, lens_ref, gate_hbm, up_hbm, down_hbm,
           out_ref, gate_v, up_v, down_v, x_in, x_parts, scaled_v, part_out, part_in, own_gu, own_ss, half_ss, inv_v,
           cross_out, cross_in, h_out, hid, acc_v, tx, outs, gram, lbuf, lens_full,
           w_sem, d_send, d_recv, x_send, x_recv, p_send, p_recv, r_send, r_recv, h_send, h_recv, t_send, t_recv,
           g_send, g_recv, l_send, l_recv):
    section = lax.axis_index("section")
    tensor = lax.axis_index("tensor")
    dp = lax.axis_index("dp")
    micros = dps * SPLIT
    width = gate_v.shape[0]
    cols = gate_v.shape[1]
    fc = cols // (2 * Q)
    rows = x_in.shape[1]
    d_model = width * dps
    half = dps // 2
    pair = 2 if tensors % 2 == 0 else 1
    lead = pair - 1
    first = tensor - lax.rem(tensor, pair)
    core = lax.rem(tensor, pair)
    side = dp // half
    hub_dp = half - 1 + side
    out_way = 2 * side - 1
    reach = (dp - hub_dp) * out_way
    is_hub = jnp.logical_and(reach == 0, core == lead)
    held = hidden_ref.shape[1]
    pw = min(held, width)
    nj = held // pw
    np_ = width // pw

    def chunk_at(which, q):
        return (side if which == 0 else 1 - side) * Q + q

    def chunk_of(j):
        return chunk_at(1, j) if j < Q else chunk_at(0, j - Q)

    def columns(c):
        return pl.ds(pl.multiple_of(c * fc, fc), fc)

    def wcopy(which, c):
        src, dst = ((gate_hbm, gate_v), (up_hbm, up_v), (down_hbm, down_v))[which]
        return pltpu.make_async_copy(src.at[0, :, columns(c)], dst.at[:, columns(c)], w_sem.at[which, c])

    for j in range(2 * Q):
        wcopy(0, chunk_of(j)).start()
        wcopy(1, chunk_of(j)).start()
    for which, q in [(w, q) for q in range(Q) for w in range(2)]:
        wcopy(2, chunk_at(which, q)).start()

    barrier = pltpu.get_barrier_semaphore()
    for kt in range(tensors):
        for kd in range(dps):
            if kt or kd:
                pl.semaphore_signal(
                    barrier, inc=1,
                    device_id={"tensor": lax.rem(tensor + kt, tensors), "dp": lax.rem(dp + kd, dps)},
                    device_id_type=MESH)

    @pl.when(section > 0)
    def _():
        for k in range(tensors):
            pl.semaphore_signal(barrier, inc=1, device_id={"section": section - 1, "tensor": k}, device_id_type=MESH)

    @pl.when(section < sections - 1)
    def _():
        for k in range(tensors):
            pl.semaphore_signal(barrier, inc=1, device_id={"section": section + 1, "tensor": k}, device_id_type=MESH)

    pl.semaphore_wait(
        barrier,
        tensors * dps - 1 + jnp.where(section == 0, 0, tensors) + jnp.where(section == sections - 1, 0, tensors))

    each = lens_ref.shape[0]
    sents = each * dps
    peers = [lax.rem(dp + k, dps) for k in range(1, dps)]
    slot = lax.broadcasted_iota(jnp.int32, lbuf.shape[1:], 0)
    own_lens = jnp.ones(lbuf.shape[1:], F32)
    for n in range(each):
        own_lens = jnp.where(slot == n, lens_ref[n].astype(F32), own_lens)
    lbuf[dp] = own_lens

    def s_copy(buf, send, recv, c, peer):
        return pltpu.make_async_remote_copy(
            src_ref=buf.at[c], dst_ref=buf.at[c], send_sem=send.at[peer], recv_sem=recv.at[c],
            device_id={"dp": peer}, device_id_type=MESH)

    def spread(m, j, k):
        h = lax.rem(m, SPLIT)
        at = tensor * held + j * pw
        piece = lax.rem(at, width) // pw
        return pltpu.make_async_remote_copy(
            src_ref=hidden_ref.at[pl.ds(pl.multiple_of(h * rows, rows), rows), pl.ds(j * pw, pw)],
            dst_ref=x_in.at[m, :, pl.ds(pl.multiple_of(piece * pw, pw), pw)],
            send_sem=d_send.at[h, j * tensors + k], recv_sem=d_recv.at[m, piece],
            device_id={"tensor": lax.rem(tensor + k, tensors), "dp": at // width}, device_id_type=MESH)

    def spread_all(m, act):
        @pl.when(jnp.logical_and(section == 0, m // SPLIT == dp))
        def _():
            for j in range(nj):
                at = tensor * held + j * pw
                for k in range(tensors):
                    if k:
                        act(m, j, k)
                    else:
                        @pl.when(at // width != dp)
                        def _():
                            act(m, j, k)

    def spread_start(m):
        spread_all(m, lambda m, j, k: spread(m, j, k).start())

        @pl.when(jnp.logical_and(section == 0, m // SPLIT == dp))
        def _():
            h = lax.rem(m, SPLIT)
            for j in range(nj):
                at = tensor * held + j * pw
                piece = lax.rem(at, width) // pw

                @pl.when(at // width == dp)
                def _():
                    x_in[m, :, pl.ds(pl.multiple_of(piece * pw, pw), pw)] = hidden_ref[
                        pl.ds(pl.multiple_of(h * rows, rows), rows), j * pw:(j + 1) * pw]

    def early(m, carry):
        spread_start(m)
        return carry

    lax.fori_loop(0, AHEAD, early, 0)
    for c in peers:
        s_copy(lbuf, l_send, l_recv, dp, c).start()

    def p_part(ref, j):
        return ref.at[:, pl.ds(0, 2 * fc + LANES)] if j == 0 else ref.at[:, pl.ds(0, 2 * fc)]

    def p_copy(m, j):
        at = reach * pair + core
        return pltpu.make_async_remote_copy(
            src_ref=p_part(part_out.at[m, j], j), dst_ref=p_part(part_in.at[m, at, j], j),
            send_sem=p_send.at[m, j], recv_sem=p_recv.at[m, at * 2 * Q + j],
            device_id={"dp": hub_dp, "tensor": first + lead}, device_id_type=MESH)

    def p_wait(m, at, j):
        ref = p_part(part_in.at[m, at, j], j)
        pltpu.make_async_remote_copy(
            src_ref=ref, dst_ref=ref, send_sem=p_send.at[m, j], recv_sem=p_recv.at[m, at * 2 * Q + j],
            device_id={"dp": 1 - side}, device_id_type=MESH).wait_recv()

    def r_copy(m, k, q):
        j = 0 if q == 0 and k == lead else 1
        return pltpu.make_async_remote_copy(
            src_ref=p_part(cross_out.at[m, k, q], j), dst_ref=p_part(cross_in.at[m, k, q], j),
            send_sem=r_send.at[m, k * Q + q], recv_sem=r_recv.at[m, k * Q + q],
            device_id={"dp": hub_dp - out_way}, device_id_type=MESH)

    targets = [dp - out_way * r for r in range(half, 0, -1)] + [dp + out_way * r for r in range(1, half)]

    def h_copy(m, k, q, n):
        to = {"dp": targets[n], "tensor": first + k} if n < dps - 1 else {"tensor": first + k}
        return pltpu.make_async_remote_copy(
            src_ref=h_out.at[m, k, q], dst_ref=hid.at[m, side * Q + q],
            send_sem=h_send.at[m, (k * Q + q) * dps + n], recv_sem=h_recv.at[m, side * Q + q],
            device_id=to, device_id_type=MESH)

    def h_wait(m, c):
        pltpu.make_async_remote_copy(
            src_ref=hid.at[m, c], dst_ref=hid.at[m, c], send_sem=h_send.at[m, 0], recv_sem=h_recv.at[m, c],
            device_id={"dp": 1 - side}, device_id_type=MESH).wait_recv()

    def h_sends(k):
        return range(dps - 1 if k == lead else dps)

    def t_copy(m, t, peer):
        return pltpu.make_async_remote_copy(
            src_ref=tx.at[m, t], dst_ref=tx.at[m, t],
            send_sem=t_send.at[m, peer], recv_sem=t_recv.at[m, t],
            device_id={"tensor": peer}, device_id_type=MESH)

    def x_copy(m, t, k, to):
        return pltpu.make_async_remote_copy(
            src_ref=tx.at[m, t], dst_ref=x_parts.at[m, t],
            send_sem=x_send.at[m, k], recv_sem=x_recv.at[m, t],
            device_id={"section": to, "tensor": k}, device_id_type=MESH)

    lane = lax.broadcasted_iota(jnp.int32, (rows, LANES), 1)

    def pack(ss):
        high = ss.astype(BF16)
        low = (ss - high.astype(F32)).astype(BF16)
        return jnp.where(lane < LANES // 2, high.astype(F32), low.astype(F32)).astype(BF16)

    def unpack(lanes):
        return jnp.sum(lanes.astype(F32), axis=1, keepdims=True) * (2.0 / LANES)

    def enter(m):
        @pl.when(section == 0)
        def _():
            for piece in range(np_):
                source = (dp * width + piece * pw) // held

                @pl.when(jnp.logical_not(jnp.logical_and(m // SPLIT == dp, source == tensor)))
                def _():
                    ref = x_in.at[m, :, pl.ds(piece * pw, pw)]
                    pltpu.make_async_remote_copy(
                        src_ref=ref, dst_ref=ref, send_sem=d_send.at[0, 0], recv_sem=d_recv.at[m, piece],
                        device_id={"dp": 1 - side}, device_id_type=MESH).wait_recv()

        @pl.when(section > 0)
        def _():
            total = None
            for t in range(tensors):
                x_copy(m, t, 0, 0).wait_recv()
                term = x_parts[m, t].astype(F32)
                total = term if total is None else total + term
            x_in[m] = total.astype(BF16)

        x = x_in[m].astype(F32)
        own_ss[m] = jnp.broadcast_to(jnp.sum(x * x, axis=1, keepdims=True), (rows, LANES))
        scaled_v[...] = (x * gain_ref[:, pl.ds(pl.multiple_of(dp * width, width), width)]).astype(BF16)

    def project(m, hub, js):
        if js[0] == 0:
            enter(m)
        for j in js:
            c = chunk_of(j)

            @pl.when(m == 0)
            def _():
                wcopy(0, c).wait()
                wcopy(1, c).wait()

            g = jnp.dot(scaled_v[...], gate_v[:, columns(c)], preferred_element_type=F32)
            u = jnp.dot(scaled_v[...], up_v[:, columns(c)], preferred_element_type=F32)
            if hub:
                own_gu[m, j, :, 0:fc] = g
                own_gu[m, j, :, fc:2 * fc] = u
            else:
                part_out[m, j, :, 0:fc] = g.astype(BF16)
                part_out[m, j, :, fc:2 * fc] = u.astype(BF16)
                if j == 0:
                    part_out[m, j, :, 2 * fc:2 * fc + LANES] = pack(own_ss[m][:, 0:1])
                p_copy(m, j).start()

    def sources(k):
        return [r * pair + k for r in range(half) if r or k != lead]

    def gathered(m, k, j):
        total = own_gu[m, j] if k == lead else None
        for at in sources(k):
            term = part_in[m, at, j, :, 0:2 * fc].astype(F32)
            total = term if total is None else total + term
        return total

    def combine(m, q):
        for k in reversed(range(pair)):
            for at in sources(k):
                p_wait(m, at, q)
            cross_out[m, k, q, :, 0:2 * fc] = gathered(m, k, q).astype(BF16)
            if q == 0 and k == lead:
                ss = own_ss[m][:, 0:1]
                for at in sources(k):
                    ss = ss + unpack(part_in[m, at, 0, :, 2 * fc:2 * fc + LANES])
                half_ss[m] = jnp.broadcast_to(ss, (rows, LANES))
                cross_out[m, k, q, :, 2 * fc:2 * fc + LANES] = pack(ss)
            r_copy(m, k, q).start()

    def activate(m, q):
        for k in reversed(range(pair)):
            for at in sources(k):
                p_wait(m, at, Q + q)
            r_copy(m, k, q).wait_recv()
            if q == 0 and k == lead:
                ss = half_ss[m][:, 0:1] + unpack(cross_in[m, k, 0, :, 2 * fc:2 * fc + LANES])
                inv_v[m] = jnp.broadcast_to(lax.rsqrt(ss * (1.0 / d_model) + RMS_EPS), (rows, LANES))
            gu = (gathered(m, k, Q + q) + cross_in[m, k, q, :, 0:2 * fc].astype(F32)) * inv_v[m][:, 0:1]
            g = gu[:, 0:fc]
            made = (g / (1.0 + jnp.exp(-g)) * gu[:, fc:2 * fc]).astype(BF16)
            h_out[m, k, q] = made
            for n in h_sends(k):
                h_copy(m, k, q, n).start()
            if k == lead:
                hid[m, side * Q + q] = made

    def descend(m, hub, parts):
        acc = None if parts[0] == (0, 0) else acc_v[m]
        for which, q in parts:
            c = chunk_at(which, q)
            if not (hub and which == 0):
                h_wait(m, c)

            @pl.when(m == 0)
            def _():
                wcopy(2, c).wait()

            term = lax.dot_general(hid[m, c], down_v[:, columns(c)], CONTRACT_LAST, preferred_element_type=F32)
            acc = term if acc is None else acc + term
        if parts[-1] != (1, Q - 1):
            acc_v[m] = acc
        else:
            tx[m, tensor] = (acc + x_in[m].astype(F32) * (1.0 / tensors)).astype(BF16)

            @pl.when(section < sections - 1)
            def _():
                for k in range(tensors):
                    x_copy(m, tensor, k, section + 1).start()

            for k in range(1, tensors):
                t_copy(m, tensor, lax.rem(tensor + k, tensors)).start()

    def settle(m):
        for k in range(1, tensors):
            other = lax.rem(tensor + k, tensors)
            t_copy(m, other, other).wait_recv()
        total = tx[m, 0].astype(F32)
        for t in range(1, tensors):
            total = total + tx[m, t].astype(F32)
        outs[m] = total.astype(BF16)

    def run(plan, hub):
        def step(i, carry):
            spread_next = i + AHEAD

            @pl.when(spread_next < micros)
            def _():
                spread_start(spread_next)

            for op, arg, lag in plan:
                m = i - lag

                @pl.when(jnp.logical_and(m >= 0, m < micros))
                def _():
                    if op == "G":
                        project(m, hub, arg)
                    elif op == "C":
                        combine(m, arg)
                    elif op == "A":
                        activate(m, arg)
                    elif op == "F":
                        descend(m, hub, arg)
                    else:
                        settle(m)
            return carry

        lax.fori_loop(0, micros + max(lag for _, _, lag in plan), step, 0)

    @pl.when(is_hub)
    def _():
        run(HUB, True)

        def drain(m, carry):
            for k in range(pair):
                for q in range(Q):
                    r_copy(m, k, q).wait_send()
                    for n in h_sends(k):
                        h_copy(m, k, q, n).wait_send()
            return carry

        lax.fori_loop(0, micros, drain, 0)

    @pl.when(jnp.logical_not(is_hub))
    def _():
        run(LEAF, False)

        def drain(m, carry):
            for j in range(2 * Q):
                p_copy(m, j).wait_send()
            return carry

        lax.fori_loop(0, micros, drain, 0)

    for c in peers:
        s_copy(lbuf, l_send, l_recv, c, c).wait_recv()
    for c in range(dps):
        lens_full[c * each:(c + 1) * each] = lbuf[c, 0:each]
    tokens = micros * rows
    per = tokens // sents
    place = lax.broadcasted_iota(jnp.int32, (sents, tokens), 1) - per * lax.broadcasted_iota(
        jnp.int32, (sents, tokens), 0)
    lens = lens_full[:, 0:1]
    valid = jnp.logical_and(place >= 0, place.astype(F32) < lens)
    mask = jnp.where(valid, 1.0, 0.0).astype(BF16)
    pooled = jnp.dot(mask, outs[...].reshape(tokens, width), preferred_element_type=F32) / lens

    def share(buf, send, recv):
        for c in peers:
            s_copy(buf, send, recv, dp, c).start()
        for c in peers:
            s_copy(buf, send, recv, c, c).wait_recv()

    mean = jnp.sum(pooled, axis=1, keepdims=True) * (1.0 / width)
    centered = pooled - mean
    narrow = centered.astype(BF16)
    sq = jnp.sum(centered * centered, axis=1, keepdims=True)
    gram[dp, 0] = jnp.zeros((sents, LANES), F32)
    gram[dp, 0, :, 0:sents] = lax.dot_general(narrow, narrow, CONTRACT_LAST, preferred_element_type=F32)
    gram[dp, 1] = jnp.broadcast_to(sq, (sents, LANES))
    gram[dp, 2] = jnp.broadcast_to(mean, (sents, LANES))
    share(gram, g_send, g_recv)
    products, sq, mean = gram[0, 0], gram[0, 1], gram[0, 2]
    for c in range(1, dps):
        products = products + gram[c, 0]
        sq = sq + gram[c, 1]
        mean = mean + gram[c, 2]
    mean = mean * (1.0 / dps)
    r_i = lax.broadcasted_iota(jnp.int32, (sents, LANES), 0)
    c_i = lax.broadcasted_iota(jnp.int32, (sents, LANES), 1)
    for c in range(dps):
        off = gram[c, 2] - mean
        off_row = jnp.sum(jnp.where(r_i == c_i, off, 0.0), axis=0, keepdims=True)
        products = products + off * off_row * float(width)
        sq = sq + off * off * float(width)
    scale = lax.rsqrt(sq * (1.0 / d_model) + UNIT_FLOOR)
    across = jnp.sum(jnp.where(r_i == c_i, scale, 0.0), axis=0, keepdims=True)
    whole = 1.0 - products * scale * across * (1.0 / d_model)
    for r in range(each):
        row = jnp.sum(jnp.where(r_i == dp * each + r, whole, 0.0), axis=0, keepdims=True)
        out_ref[0, r:r + 1, :] = row[:, 0:sents]

    def drain(m, carry):
        spread_all(m, lambda m, j, k: spread(m, j, k).wait_send())
        for k in range(1, tensors):
            t_copy(m, tensor, lax.rem(tensor + k, tensors)).wait_send()

        @pl.when(section < sections - 1)
        def _():
            for k in range(tensors):
                x_copy(m, tensor, k, section + 1).wait_send()
        return carry

    lax.fori_loop(0, micros, drain, 0)
    for c in peers:
        s_copy(lbuf, l_send, l_recv, dp, c).wait_send()
        s_copy(gram, g_send, g_recv, dp, c).wait_send()


def per_device(hidden_in, norm_gain, gate_weight, up_weight, down_weight, lengths):
    sections = lax.axis_size("section")
    tensors = lax.axis_size("tensor")
    dps = lax.axis_size("dp")
    _, width, cols = gate_weight.shape
    micros = dps * SPLIT
    rows = hidden_in.shape[0] // SPLIT
    fc = cols // (2 * Q)
    half = dps // 2
    pair = 2 if tensors % 2 == 0 else 1
    held = hidden_in.shape[1]
    pw = min(held, width)
    each = lengths.shape[0]
    sents = each * dps
    vm = pl.BlockSpec(memory_space=pltpu.VMEM)
    hbm = pl.BlockSpec(memory_space=pl.ANY)
    dma = pltpu.SemaphoreType.DMA
    smem = pl.BlockSpec(memory_space=pltpu.SMEM)
    return pl.pallas_call(
        functools.partial(kernel, dps, tensors, sections),
        out_shape=jax.ShapeDtypeStruct((1, each, sents), F32),
        in_specs=[vm] * 2 + [smem] + [hbm] * 3,
        out_specs=vm,
        scratch_shapes=[
            pltpu.VMEM((width, cols), BF16),
            pltpu.VMEM((width, cols), BF16),
            pltpu.VMEM((width, cols), BF16),
            pltpu.VMEM((micros, rows, width), BF16),
            pltpu.VMEM((micros, tensors, rows, width), BF16),
            pltpu.VMEM((rows, width), BF16),
            pltpu.VMEM((micros, 2 * Q, rows, 2 * fc + LANES), BF16),
            pltpu.VMEM((micros, half * pair, 2 * Q, rows, 2 * fc + LANES), BF16),
            pltpu.VMEM((micros, 2 * Q, rows, 2 * fc), F32),
            pltpu.VMEM((micros, rows, LANES), F32),
            pltpu.VMEM((micros, rows, LANES), F32),
            pltpu.VMEM((micros, rows, LANES), F32),
            pltpu.VMEM((micros, pair, Q, rows, 2 * fc + LANES), BF16),
            pltpu.VMEM((micros, pair, Q, rows, 2 * fc + LANES), BF16),
            pltpu.VMEM((micros, pair, Q, rows, fc), BF16),
            pltpu.VMEM((micros, 2 * Q, rows, fc), BF16),
            pltpu.VMEM((micros, rows, width), F32),
            pltpu.VMEM((micros, tensors, rows, width), BF16),
            pltpu.VMEM((micros, rows, width), BF16),
            pltpu.VMEM((dps, 3, sents, LANES), F32),
            pltpu.VMEM((dps, -(-each // 8) * 8, LANES), F32),
            pltpu.VMEM((sents, LANES), F32),
            dma((3, 2 * Q)),
            dma((SPLIT, held // pw * tensors)),
            dma((micros, width // pw)),
            dma((micros, tensors)),
            dma((micros, tensors)),
            dma((micros, 2 * Q)),
            dma((micros, half * pair * 2 * Q)),
            dma((micros, pair * Q)),
            dma((micros, pair * Q)),
            dma((micros, pair * Q * dps)),
            dma((micros, 2 * Q)),
            dma((micros, tensors)),
            dma((micros, tensors)),
            dma((dps,)),
            dma((dps,)),
            dma((dps,)),
            dma((dps,)),
        ],
        compiler_params=pltpu.CompilerParams(
            collective_id=0, has_side_effects=True, vmem_limit_bytes=60 * 1024 * 1024),
    )(hidden_in, norm_gain, lengths, gate_weight, up_weight, down_weight)


def solution(mesh):
    placed = (
        P("dp", "tensor"),
        P("section", None),
        P("section", "dp", "tensor"),
        P("section", "dp", "tensor"),
        P("section", "dp", "tensor"),
        P("dp"),
    )
    return jax.shard_map(
        per_device, mesh=mesh, in_specs=placed, out_specs=P("section", "dp", None), check_vma=False
    )
```

time: 152 us -> 144 us (0.947)
  Pallas kernels: 150 us -> 142 us
    pallas_call x1, Pallas kernels: 150 us -> 142 us  [per_device(): pl.pallas_call(functools.partial(kernel, dps, tensors, sections), out_sha...]
where the time goes in v1:
time: 144 us; the launch traced here: 143 us
  Pallas kernels  142 us (99%)
    pallas_call x1, Pallas kernels, per_device(): pl.pallas_call(functools.partial(kernel, dps, tensors, sections), out_sha...  142 us

profile of v1, /device:TPU:7, one launch (start us, length us, event | category | flops | bytes accessed | tf_op | source)
XLA Modules:
  0.0 143.4 jit_solution(17107225967329204184)
XLA Ops:
  0.0 142.1 %shard_map.64 = f32[1,4,16]{2,1,0:T(4,128)} custom-call(bf16[32,2048]{1,0:T(8,128)(2,1)} %hidden_ref.1, f32[1,4096]{1,0:T(1,128)} %gain_ref.1, s32[4]{0:T(128)} %lens_ref.1, bf16[1,1024,4096]{2,1,0:T(8,128)(2,1)} %gate_hbm.1, bf16[1,1024,4096]{2,1,0:T(8,128)(2,1)} %up_hbm.1, bf16[1,1024,4096]{2,1,0:T(8,128)(2,1)} %down_hbm.1), custom_call_target="tpu_custom_call" | custom-call | tf_op jit(solution)/shard_map/pallas_call | solution.py:479
  142.2 1.3 copy.8

commit v2 on v1

--- a/solution.py
+++ b/solution.py
@@ -17,15 +17,15 @@
 
 SPLIT = 2
 Q = 2
-AHEAD = 2
-
-LEAF = (("G", (0, 1, 2, 3), 0), ("F", ((0, 0), (1, 0), (0, 1), (1, 1)), 1), ("E", None, 2))
-HUB = (("G", (0, 1), 0), ("A", 0, 1), ("G", (2, 3), 0), ("A", 1, 1), ("C", 0, 0), ("F", ((0, 0), (0, 1)), 1),
-       ("C", 1, 0), ("F", ((1, 0), (1, 1)), 1), ("E", None, 2))
+AHEAD = 8
+
+LEAF = (("G", (0, 1), 0), ("F", ((0, 1), (1, 1)), 2), ("E", None, 3), ("G", (2, 3), 0), ("F", ((0, 0), (1, 0)), 1))
+HUB = (("G", (0, 1), 0), ("F", ((1, 0), (1, 1)), 2), ("E", None, 3), ("A", 0, 1), ("G", (2, 3), 0), ("A", 1, 1),
+       ("F", ((0, 0), (0, 1)), 1), ("C", 0, 0), ("C", 1, 0))
 
 
 def kernel(dps, tensors, sections, hidden_ref, gain_ref, lens_ref, gate_hbm, up_hbm, down_hbm,
-           out_ref, gate_v, up_v, down_v, x_in, x_parts, scaled_v, part_out, part_in, own_gu, own_ss, half_ss, inv_v,
+           out_ref, gate_v, up_v, down_v, down_t, x_in, x_parts, scaled_v, part_out, part_in, own_gu, own_ss, half_ss, inv_v,
            cross_out, cross_in, h_out, hid, acc_v, tx, outs, gram, lbuf, lens_full,
            w_sem, d_send, d_recv, x_send, x_recv, p_send, p_recv, r_send, r_recv, h_send, h_recv, t_send, t_recv,
            g_send, g_recv, l_send, l_recv):
@@ -66,11 +66,11 @@
         src, dst = ((gate_hbm, gate_v), (up_hbm, up_v), (down_hbm, down_v))[which]
         return pltpu.make_async_copy(src.at[0, :, columns(c)], dst.at[:, columns(c)], w_sem.at[which, c])
 
+    for c in range(2 * Q):
+        wcopy(2, c).start()
     for j in range(2 * Q):
         wcopy(0, chunk_of(j)).start()
         wcopy(1, chunk_of(j)).start()
-    for which, q in [(w, q) for q in range(Q) for w in range(2)]:
-        wcopy(2, chunk_at(which, q)).start()
 
     barrier = pltpu.get_barrier_semaphore()
     for kt in range(tensors):
@@ -244,16 +244,16 @@
         scaled_v[...] = (x * gain_ref[:, pl.ds(pl.multiple_of(dp * width, width), width)]).astype(BF16)
 
     def project(m, hub, js):
+        @pl.when(m == 0)
+        def _():
+            for j in js:
+                wcopy(0, chunk_of(j)).wait()
+                wcopy(1, chunk_of(j)).wait()
+
         if js[0] == 0:
             enter(m)
         for j in js:
             c = chunk_of(j)
-
-            @pl.when(m == 0)
-            def _():
-                wcopy(0, c).wait()
-                wcopy(1, c).wait()
-
             g = jnp.dot(scaled_v[...], gate_v[:, columns(c)], preferred_element_type=F32)
             u = jnp.dot(scaled_v[...], up_v[:, columns(c)], preferred_element_type=F32)
             if hub:
@@ -309,15 +309,11 @@
     def descend(m, hub, parts):
         acc = None if parts[0] == (0, 0) else acc_v[m]
         for which, q in parts:
+            if not (hub and which == 0):
+                h_wait(m, chunk_at(which, q))
+        for which, q in parts:
             c = chunk_at(which, q)
-            if not (hub and which == 0):
-                h_wait(m, c)
-
-            @pl.when(m == 0)
-            def _():
-                wcopy(2, c).wait()
-
-            term = lax.dot_general(hid[m, c], down_v[:, columns(c)], CONTRACT_LAST, preferred_element_type=F32)
+            term = jnp.dot(hid[m, c], down_t[columns(c), :], preferred_element_type=F32)
             acc = term if acc is None else acc + term
         if parts[-1] != (1, Q - 1):
             acc_v[m] = acc
@@ -341,7 +337,20 @@
             total = total + tx[m, t].astype(F32)
         outs[m] = total.astype(BF16)
 
-    def run(plan, hub):
+    turn = min(fc, 2 * LANES)
+    for c in range(2 * Q):
+        wcopy(2, c).wait()
+
+        def flip(b, carry):
+            at = pl.ds(pl.multiple_of(c * fc + b * turn, turn), turn)
+            down_t[at, :] = down_v[:, at].T
+            return carry
+
+        lax.fori_loop(0, fc // turn, flip, 0)
+
+    def run(hub):
+        steps = HUB if hub else LEAF
+
         def step(i, carry):
             spread_next = i + AHEAD
 
@@ -349,7 +358,7 @@
             def _():
                 spread_start(spread_next)
 
-            for op, arg, lag in plan:
+            for op, arg, lag in steps:
                 m = i - lag
 
                 @pl.when(jnp.logical_and(m >= 0, m < micros))
@@ -366,11 +375,11 @@
                         settle(m)
             return carry
 
-        lax.fori_loop(0, micros + max(lag for _, _, lag in plan), step, 0)
+        lax.fori_loop(0, micros + max(lag for _, _, lag in steps), step, 0)
 
     @pl.when(is_hub)
     def _():
-        run(HUB, True)
+        run(True)
 
         def drain(m, carry):
             for k in range(pair):
@@ -384,7 +393,7 @@
 
     @pl.when(jnp.logical_not(is_hub))
     def _():
-        run(LEAF, False)
+        run(False)
 
         def drain(m, carry):
             for j in range(2 * Q):
@@ -485,6 +494,7 @@
             pltpu.VMEM((width, cols), BF16),
             pltpu.VMEM((width, cols), BF16),
             pltpu.VMEM((width, cols), BF16),
+            pltpu.VMEM((cols, width), BF16),
             pltpu.VMEM((micros, rows, width), BF16),
             pltpu.VMEM((micros, tensors, rows, width), BF16),
             pltpu.VMEM((rows, width), BF16),

time: 144 us -> 128 us (0.89)
  Pallas kernels: 142 us -> 127 us
    pallas_call x1, Pallas kernels: 142 us -> 127 us  [per_device(): pl.pallas_call(functools.partial(kernel, dps, tensors, sections), out_sha...]
where the time goes in v2:
time: 128 us
  Pallas kernels  127 us (99%)
    pallas_call x1, Pallas kernels, per_device(): pl.pallas_call(functools.partial(kernel, dps, tensors, sections), out_sha...  127 us

profile of v2, /device:TPU:7, one launch (start us, length us, event | category | flops | bytes accessed | tf_op | source)
XLA Modules:
  0.0 128.2 jit_solution(14179748781482055348)
XLA Ops:
  0.0 127.0 %shard_map.64 = f32[1,4,16]{2,1,0:T(4,128)} custom-call(bf16[32,2048]{1,0:T(8,128)(2,1)} %hidden_ref.1, f32[1,4096]{1,0:T(1,128)} %gain_ref.1, s32[4]{0:T(128)} %lens_ref.1, bf16[1,1024,4096]{2,1,0:T(8,128)(2,1)} %gate_hbm.1, bf16[1,1024,4096]{2,1,0:T(8,128)(2,1)} %up_hbm.1, bf16[1,1024,4096]{2,1,0:T(8,128)(2,1)} %down_hbm.1), custom_call_target="tpu_custom_call" | custom-call | tf_op jit(solution)/shard_map/pallas_call | solution.py:488
  127.0 1.3 copy.8

commit v3 on v2

--- a/solution.py
+++ b/solution.py
@@ -17,11 +17,11 @@
 
 SPLIT = 2
 Q = 2
-AHEAD = 8
-
-LEAF = (("G", (0, 1), 0), ("F", ((0, 1), (1, 1)), 2), ("E", None, 3), ("G", (2, 3), 0), ("F", ((0, 0), (1, 0)), 1))
-HUB = (("G", (0, 1), 0), ("F", ((1, 0), (1, 1)), 2), ("E", None, 3), ("A", 0, 1), ("G", (2, 3), 0), ("A", 1, 1),
-       ("F", ((0, 0), (0, 1)), 1), ("C", 0, 0), ("C", 1, 0))
+
+LEAF = (("G", (0,), 0), ("F", ((0, 0), (1, 0)), 2), ("G", (1,), 0), ("F", ((0, 1), (1, 1)), 2), ("E", None, 3),
+        ("G", (2, 3), 0))
+HUB = (("G", (0, 1), 0), ("F", ((1, 0), (1, 1)), 2), ("A", 0, 1), ("G", (2,), 0), ("A", 1, 1), ("G", (3,), 0),
+       ("C", 0, 0), ("F", ((0, 0), (0, 1)), 1), ("C", 1, 0), ("E", None, 3))
 
 
 def kernel(dps, tensors, sections, hidden_ref, gain_ref, lens_ref, gate_hbm, up_hbm, down_hbm,
@@ -151,9 +151,7 @@
         spread_start(m)
         return carry
 
-    lax.fori_loop(0, AHEAD, early, 0)
-    for c in peers:
-        s_copy(lbuf, l_send, l_recv, dp, c).start()
+    lax.fori_loop(0, micros, early, 0)
 
     def p_part(ref, j):
         return ref.at[:, pl.ds(0, 2 * fc + LANES)] if j == 0 else ref.at[:, pl.ds(0, 2 * fc)]
@@ -348,16 +346,13 @@
 
         lax.fori_loop(0, fc // turn, flip, 0)
 
+    for c in peers:
+        s_copy(lbuf, l_send, l_recv, dp, c).start()
+
     def run(hub):
         steps = HUB if hub else LEAF
 
         def step(i, carry):
-            spread_next = i + AHEAD
-
-            @pl.when(spread_next < micros)
-            def _():
-                spread_start(spread_next)
-
             for op, arg, lag in steps:
                 m = i - lag
 
@@ -425,21 +420,19 @@
     centered = pooled - mean
     narrow = centered.astype(BF16)
     sq = jnp.sum(centered * centered, axis=1, keepdims=True)
-    gram[dp, 0] = jnp.zeros((sents, LANES), F32)
-    gram[dp, 0, :, 0:sents] = lax.dot_general(narrow, narrow, CONTRACT_LAST, preferred_element_type=F32)
-    gram[dp, 1] = jnp.broadcast_to(sq, (sents, LANES))
-    gram[dp, 2] = jnp.broadcast_to(mean, (sents, LANES))
+    column = lax.broadcasted_iota(jnp.int32, (sents, LANES), 1)
+    gram[dp] = jnp.where(column == sents, sq, jnp.where(column == sents + 1, mean, 0.0))
+    gram[dp, :, 0:sents] = lax.dot_general(narrow, narrow, CONTRACT_LAST, preferred_element_type=F32)
     share(gram, g_send, g_recv)
-    products, sq, mean = gram[0, 0], gram[0, 1], gram[0, 2]
+    products = gram[0]
     for c in range(1, dps):
-        products = products + gram[c, 0]
-        sq = sq + gram[c, 1]
-        mean = mean + gram[c, 2]
-    mean = mean * (1.0 / dps)
+        products = products + gram[c]
+    sq = products[:, sents:sents + 1]
+    mean = products[:, sents + 1:sents + 2] * (1.0 / dps)
     r_i = lax.broadcasted_iota(jnp.int32, (sents, LANES), 0)
     c_i = lax.broadcasted_iota(jnp.int32, (sents, LANES), 1)
     for c in range(dps):
-        off = gram[c, 2] - mean
+        off = gram[c, :, sents + 1:sents + 2] - mean
         off_row = jnp.sum(jnp.where(r_i == c_i, off, 0.0), axis=0, keepdims=True)
         products = products + off * off_row * float(width)
         sq = sq + off * off * float(width)
@@ -511,7 +504,7 @@
             pltpu.VMEM((micros, rows, width), F32),
             pltpu.VMEM((micros, tensors, rows, width), BF16),
             pltpu.VMEM((micros, rows, width), BF16),
-            pltpu.VMEM((dps, 3, sents, LANES), F32),
+            pltpu.VMEM((dps, sents, LANES), F32),
             pltpu.VMEM((dps, -(-each // 8) * 8, LANES), F32),
             pltpu.VMEM((sents, LANES), F32),
             dma((3, 2 * Q)),

time: 128 us -> 125 us (0.977)
  Pallas kernels: 127 us -> 124 us
    pallas_call x1, Pallas kernels: 127 us -> 124 us  [per_device(): pl.pallas_call(functools.partial(kernel, dps, tensors, sections), out_sha...]
where the time goes in v3:
time: 125 us
  Pallas kernels  124 us (99%)
  local copies, waits for them, and re-layouts  1.26 us (1%)
    pallas_call x1, Pallas kernels, per_device(): pl.pallas_call(functools.partial(kernel, dps, tensors, sections), out_sha...  124 us

profile of v3, /device:TPU:7, one launch (start us, length us, event | category | flops | bytes accessed | tf_op | source)
XLA Modules:
  0.0 125.1 jit_solution(16668761829060959826)
XLA Ops:
  0.0 123.8 %shard_map.64 = f32[1,4,16]{2,1,0:T(4,128)} custom-call(bf16[32,2048]{1,0:T(8,128)(2,1)} %hidden_ref.1, f32[1,4096]{1,0:T(1,128)} %gain_ref.1, s32[4]{0:T(128)} %lens_ref.1, bf16[1,1024,4096]{2,1,0:T(8,128)(2,1)} %gate_hbm.1, bf16[1,1024,4096]{2,1,0:T(8,128)(2,1)} %up_hbm.1, bf16[1,1024,4096]{2,1,0:T(8,128)(2,1)} %down_hbm.1), custom_call_target="tpu_custom_call" | custom-call | tf_op jit(solution)/shard_map/pallas_call | solution.py:481
  123.8 1.3 %copy.8 = f32[1,4,16]{2,1,0:T(4,128)} copy(f32[1,4,16]{2,1,0:T(4,128)} %shard_map.64) | data formatting | bytes 512
